TPU v7x, 32 devices: a whole 2x2x4 slice. The times are simulated.
32 devices in a mesh: seq: 16 (over z, y, x), tensor: 2 (over core).
Axes of the slice: x: 2, y: 2, z: 4, core: 2. Of those that a mesh axis runs over, the one named last changes fastest.
Arguments:
- hidden: bfloat16 [2, 4096, 8192], P(None, 'seq', 'tensor'), may hold values from -160 to 160
- norm_gain: bfloat16 [8192], P('tensor'), may hold values from 0.25 to 1.75
- value_weight: bfloat16 [8192], P('tensor'), may hold values from -0.0625 to 0.0625
- rewards: float32 [2, 4096], P(None, 'seq'), may hold values from -6 to 6
- done_flags: int32 [2, 4096], P(None, 'seq'), may hold values 0 or 1
- valid_mask: int32 [2, 4096], P('tensor', 'seq'), may hold values 0 or 1
- new_logprob: float32 [2, 4096], P('tensor', 'seq'), may hold values from -1 to 1
- old_logprob: float32 [2, 4096], P('tensor', 'seq'), may hold values from -1 to 1
- discount: float32 [2], replicated, may hold values from 0.9 to 1
- trace_decay: float32 [2], replicated, may hold values from 0.9 to 1
- bootstrap: float32 [2], replicated, may hold values from -5 to 5
Outputs:
- values: float32 [2, 4096], P('tensor', 'seq')
- white_adv: float32 [2, 4096], P('tensor', 'seq')
- token_loss: float32 [2, 4096], P('tensor', 'seq')
- policy_loss: float32 [], replicated
All inputs are finite; a program needn't handle non-finite values. No bound on the sum of `done_flags` or of `valid_mask` on one device may be relied on, other than what follows from the above.
Results may differ from a plain program's by a relative error of at most 0.00035.
Values sent between devices are 32-bit elements; how exact they have to be, the bound alone decides.
A program may use at most 64 MiB of HBM per device.

v0:
```python
import jax
import jax.numpy as jnp
from jax import lax
from jax.sharding import PartitionSpec as P

H = 8192
EPS_NORM = 1e-06
EPS_WHITE = 1e-08
CLIP = 0.2
HIGHEST = lax.Precision.HIGHEST


def compose(earlier, later):
    return (later[0] + later[1] * earlier[0], later[1] * earlier[1])


def local_pass(values, rewards, done_flags, discount, trace_decay):
    row_count, length = values.shape
    alive = 1.0 - done_flags.astype(jnp.float32)
    inner_next = jnp.concatenate([values[:, 1:], jnp.zeros((row_count, 1), jnp.float32)], axis=1)
    delta = rewards + discount[:, None] * alive * inner_next - values
    decay = discount * trace_decay
    counted = jnp.cumsum(done_flags, axis=1) - done_flags
    later_pos = lax.broadcasted_iota(jnp.int32, (length, length), 1)
    early_pos = lax.broadcasted_iota(jnp.int32, (length, length), 0)
    upper = later_pos >= early_pos
    distance = jnp.maximum(later_pos - early_pos, 0).astype(jnp.float32)
    powers = jnp.exp(distance[None, :, :] * jnp.log(decay)[:, None, None])
    same_episode = counted[:, None, :] == counted[:, :, None]
    weights = jnp.where(upper[None, :, :] & same_episode, powers, 0.0)
    local_adv = jnp.einsum(
        "stj,sj->st", weights, delta, precision=HIGHEST, preferred_element_type=jnp.float32
    )
    coef = weights[:, :, length - 1] * (discount * alive[:, length - 1])[:, None]
    return (local_adv, coef)


def fold_step(carry, block):
    return (compose(carry, block), carry)


def shards(
    hidden,
    norm_gain,
    value_weight,
    rewards,
    done_flags,
    valid_mask,
    new_logprob,
    old_logprob,
    discount,
    trace_decay,
    bootstrap,
):
    seqs_all = hidden.shape[0]
    own_rows = seqs_all // lax.axis_size("tensor")
    first_row = lax.axis_index("tensor") * own_rows
    scaled = norm_gain.astype(jnp.float32) * value_weight.astype(jnp.float32)
    squares = jnp.einsum("sth,sth->st", hidden, hidden, preferred_element_type=jnp.float32)
    products = jnp.einsum(
        "sth,h->st", hidden, scaled, precision=HIGHEST, preferred_element_type=jnp.float32
    )
    squares, products = (
        lax.psum_scatter(squares, "tensor", scatter_dimension=0, tiled=True),
        lax.psum_scatter(products, "tensor", scatter_dimension=0, tiled=True),
    )
    values = products * lax.rsqrt(squares / H + EPS_NORM)

    def pick(array):
        return lax.dynamic_slice_in_dim(array, first_row, own_rows, 0)

    rewards_rows = pick(rewards)
    flags_rows = pick(done_flags)
    discount_rows = pick(discount)
    trace_rows = pick(trace_decay)
    local_adv, coef = local_pass(values, rewards_rows, flags_rows, discount_rows, trace_rows)
    weight = valid_mask.astype(jnp.float32)
    offset = values[:, 0] + trace_rows * local_adv[:, 0]
    slope = trace_rows * coef[:, 0]
    packed = jnp.stack(
        [
            offset,
            slope,
            jnp.sum(weight, axis=1),
            jnp.sum(weight * local_adv, axis=1),
            jnp.sum(weight * coef, axis=1),
            jnp.sum(weight * local_adv * local_adv, axis=1),
            jnp.sum(weight * local_adv * coef, axis=1),
            jnp.sum(weight * coef * coef, axis=1),
        ],
        axis=1,
    )
    gathered = lax.all_gather(packed[None], ("seq", "tensor"), axis=0, tiled=True)
    seq_count = lax.axis_size("seq")
    table = gathered.reshape(seq_count, seqs_all, 8)
    start_pair = (jnp.zeros((seqs_all,), jnp.float32), jnp.ones((seqs_all,), jnp.float32))
    _, prefix = lax.scan(fold_step, start_pair, (table[:, :, 0], table[:, :, 1]), reverse=True)
    entering = prefix[0] + prefix[1] * bootstrap[None, :]
    count = jnp.sum(table[:, :, 2])
    total = jnp.sum(table[:, :, 3] + entering * table[:, :, 4])
    square_sum = jnp.sum(
        table[:, :, 5] + 2.0 * entering * table[:, :, 6] + entering * entering * table[:, :, 7]
    )
    mean = total / count
    variance = square_sum / count - mean * mean
    own_entering = lax.dynamic_slice_in_dim(
        lax.dynamic_index_in_dim(entering, lax.axis_index("seq"), 0, False), first_row, own_rows, 0
    )
    adv_own = local_adv + coef * own_entering[:, None]
    white_adv = (adv_own - mean) * lax.rsqrt(variance + EPS_WHITE)
    ratio = jnp.exp(new_logprob - old_logprob)
    surrogate = jnp.minimum(ratio * white_adv, jnp.clip(ratio, 1.0 - CLIP, 1.0 + CLIP) * white_adv)
    token_loss = -weight * surrogate
    loss_sum = lax.psum(jnp.sum(token_loss), ("seq", "tensor"))
    policy_loss = loss_sum / count
    return (values, white_adv, token_loss, policy_loss)


def solution(mesh):
    in_specs = (
        P(None, "seq", "tensor"),
        P("tensor"),
        P("tensor"),
        P(None, "seq"),
        P(None, "seq"),
        P("tensor", "seq"),
        P("tensor", "seq"),
        P("tensor", "seq"),
        P(),
        P(),
        P(),
    )
    out_specs = (P("tensor", "seq"), P("tensor", "seq"), P("tensor", "seq"), P())
    return jax.shard_map(shards, mesh=mesh, in_specs=in_specs, out_specs=out_specs, check_vma=False)
```

profile of v0, /device:TPU:12, one launch (start us, length us, event | category | flops | bytes accessed | tf_op | source)
XLA Modules:
  0.0 122.1 jit_solution(13526523173218547624)
XLA Ops:
  0.6 0.0 copy-start
  0.6 0.9 convert_multiply_fusion.1
  1.5 0.0 copy-start.11
  1.5 0.0 copy-start.9
  1.5 0.0 copy-start.6
  1.5 0.0 copy-start.10
  1.5 0.0 copy-start.3
  1.5 0.0 copy-start.8
  1.6 0.0 copy-start.7
  1.6 0.0 copy-start.4
  1.6 0.0 copy-start.5
  1.6 6.0 %fusion.45 = f32[1,2,256]{2,0,1:T(1,128)S(1)} fusion(f32[4096,1,1]{0,1,2:T(1,128)S(1)} %bitcast.83, bf16[2,256,4096]{2,1,0:T(8,128)(2,1)} %param.13), kind=kOutput, calls=%fused_computation.75 | convolution fusion | flops 25165824 | bytes 4212736 | tf_op jit(solution)/shard_map/sth,h->st/dot_general | solution.py:60
  7.6 0.0 copy-done
  7.6 0.9 fusion.3
  8.5 2.5 %all-reduce.2 = (f32[2,256]{1,0:T(2,128)S(1)}, f32[2,256]{1,0:T(2,128)S(1)}) all-reduce(f32[2,256]{1,0:T(2,128)S(1)} %bitcast.85, f32[2,256]{1,0:T(2,128)S(1)} %fusion.3), channel_id=3, replica_groups=mesh['seq'=16,'tensor'=2] {'tensor'}, use_global_device_ids=true, to_apply=%region_0.0.clone | all-reduce | flops 1024 | bytes 8192
  11.0 0.0 copy-done.11
  11.0 0.6 dynamic-slice.1
  11.5 0.7 dynamic-slice_multiply_fusion.1
  12.2 0.0 copy-start.1
  12.2 0.0 copy-done.9
  12.2 0.6 dynamic_slice.37
  12.8 0.0 copy-done.6
  12.8 0.6 slice.66
  14.7 0.0 copy-done.10
  14.7 0.6 dynamic_slice.38
  16.6 0.3 reduce-window.6
  17.0 0.2 slice_reduce_fusion.1
  17.1 0.2 reduce-window.9
  17.3 0.1 broadcast.116
  17.4 0.6 slice.65
  18.0 0.1 slice.64
  18.1 0.0 copy-done.3
  18.1 0.0 copy-done.8
  18.1 2.3 %multiply_reduce_fusion = (f32[]{:T(128)}, f32[]{:T(128)}, f32[]{:T(128)}, f32[]{:T(128)}, f32[]{:T(128)}, /*index=5*/f32[]{:T(128)}, f32[1,256,1]{1,2,0:T(1,128)S(1)}, f32[1,256]{1,0:T(1,128)S(1)}) fusion(s32[1,256]{1,0:T(1,128)S(1)} %copy-done.3, f32[]{:T(128)} %bitcast.13, f32[]{:T(128)} %bitcast.7, s32[256]{0:T(256)S(1)} %bitcast.96, s32[1]{0:T(128)} %slice.65, ...), kind=kOutput, calls=%fused_computation.56 | convolution fusion | flops 1318138 | bytes 13340 | tf_op jit(solution)/shard_map/stj,sj->st/dot_general | solution.py:31
  20.4 0.5 slice.67
  20.9 0.5 slice.68
  23.4 0.5 slice.69
  25.2 3.8 %stack.35 = f32[1,8]{1,0:T(1,128)S(1)} concatenate(f32[1,1]{1,0:T(1,128)} %bitcast.16, f32[1,1]{1,0:T(1,128)} %bitcast.19, f32[1,1]{1,0:T(1,128)} %bitcast.20, f32[1,1]{1,0:T(1,128)} %bitcast.21, f32[1,1]{1,0:T(1,128)} %bitcast.22, f32[1,1]{1,0:T(1,128)} %bitcast.23, f32[1,1]{1,0:T(1,128)} %bitcast.24, f32[1,1]{1,0:T(1,128)} %bitcast.25), dimensions={1} | concatenate | bytes 64 | tf_op jit(solution)/shard_map/stack | solution.py:80
  29.0 31.7 %all-gather.1 = f32[32,1,8]{2,1,0:T(1,128)S(1)} all-gather(f32[1,1,8]{2,1,0:T(1,128)S(1)} %bitcast.92), channel_id=2, replica_groups=mesh['seq'=16,'tensor'=2] {'seq','tensor'}, dimensions={0}, use_global_device_ids=true | all-gather | bytes 1056 | tf_op jit(solution)/shard_map/all_gather | solution.py:93
  60.7 0.7 slice_reduce_fusion
  61.4 0.1 copy.56
  61.5 0.1 copy.55
  61.6 0.1 copy.59
  61.7 0.1 copy.58
  61.8 0.1 copy.57
  61.9 0.1 copy.53
  62.0 0.1 copy.39
  62.1 0.1 copy.54
  62.2 0.1 copy.40
  62.3 1.9 %while.21 = (s32[]{:T(128)}, f32[2]{0:T(128)S(1)}, f32[2]{0:T(128)S(1)}, f32[16,2]{1,0:T(8,128)S(1)}, f32[16,2]{1,0:T(8,128)S(1)}, /*index=5*/f32[16,2]{1,0:T(8,...) while((s32[]{:T(128)}, f32[2]{0:T(128)S(1)}, f32[2]{0:T(128)S(1)}, ...), condition=%wide.region_11.12_spmd.clone, body=%wide.region_10.11_spmd.clone.sunk | while | flops 14 | bytes 239 | solution.py:97
  64.2 0.1 copy.42
  64.3 0.1 copy.41
  64.3 0.0 copy-done.7
  64.3 0.7 fusion.34
  65.0 0.7 dynamic_slice.40
  65.7 0.7 broadcast_multiply_fusion
  69.1 0.0 copy-start.2
  69.1 0.0 copy-done.4
  69.1 0.0 copy-done.5
  69.1 1.3 %fusion.43 = (f32[]{:T(128)}, f32[1,256]{1,0:T(1,128)}) fusion(f32[1,256]{1,0:T(1,128)S(1)} %bitcast.90, f32[1,256]{1,0:T(1,128)S(1)} %copy-done.4, f32[1,256]{1,0:T(1,128)S(1)} %copy-done.5, s32[1,256]{1,0:T(1,128)S(1)} %copy-done.3), kind=kLoop, calls=%fused_computation.74 | loop fusion | flops 2303 | bytes 5124 | tf_op jit(solution)/shard_map/reduce_sum | solution.py:114
  70.4 49.3 %psum.7 = f32[]{:T(128)} all-reduce(f32[]{:T(128)} %get-tuple-element.217), channel_id=1, replica_groups=mesh['seq'=16,'tensor'=2] {'seq','tensor'}, use_global_device_ids=true, to_apply=%region_16.17 | all-reduce | flops 1 | bytes 8 | tf_op jit(solution)/shard_map/psum | solution.py:114
  121.0 0.0 copy-done.1
  121.0 0.0 copy-done.2
  (57 shorter events, 1.6 us)
Async XLA Ops:
  0.6 6.9 %copy-start = (bf16[2,256,4096]{2,1,0:T(8,128)(2,1)S(1)}, bf16[2,256,4096]{2,1,0:T(8,128)(2,1)}, u32[]{:S(2)}) copy-start(bf16[2,256,4096]{2,1,0:T(8,128)(2,1)} %param.13) | copy-start | bytes 12582916
  1.5 9.4 %copy-start.11 = (u32[32]{0:T(128)S(1)}, u32[32]{0:T(128)}, u32[]{:S(2)}) copy-start(u32[32]{0:T(128)} %constant.101) | copy-start | bytes 388
  1.5 10.7 %copy-start.9 = (f32[2]{0:T(128)S(1)}, f32[2]{0:T(128)}, u32[]{:S(2)}) copy-start(f32[2]{0:T(128)} %param.21) | copy-start | bytes 28
  1.5 11.3 %copy-start.6 = (s32[2,256]{1,0:T(2,128)S(1)}, s32[2,256]{1,0:T(2,128)}, u32[]{:S(2)}) copy-start(s32[2,256]{1,0:T(2,128)} %param.17) | copy-start | bytes 6148
  1.5 13.2 %copy-start.10 = (f32[2]{0:T(128)S(1)}, f32[2]{0:T(128)}, u32[]{:S(2)}) copy-start(f32[2]{0:T(128)} %param.22) | copy-start | bytes 28
  1.5 16.5 %copy-start.3 = (s32[1,256]{1,0:T(1,128)S(1)}, s32[1,256]{1,0:T(1,128)}, u32[]{:S(2)}) copy-start(s32[1,256]{1,0:T(1,128)} %param.18) | copy-start | bytes 3076
  1.5 16.5 %copy-start.8 = (f32[2,256]{1,0:T(2,128)S(1)}, f32[2,256]{1,0:T(2,128)}, u32[]{:S(2)}) copy-start(f32[2,256]{1,0:T(2,128)} %param.16) | copy-start | bytes 6148
  1.6 62.8 %copy-start.7 = (f32[2]{0:T(128)S(1)}, f32[2]{0:T(128)}, u32[]{:S(2)}) copy-start(f32[2]{0:T(128)} %param.23) | copy-start | bytes 28
  1.6 67.5 %copy-start.4 = (f32[1,256]{1,0:T(1,128)S(1)}, f32[1,256]{1,0:T(1,128)}, u32[]{:S(2)}) copy-start(f32[1,256]{1,0:T(1,128)} %param.19) | copy-start | bytes 3076
  1.6 67.5 %copy-start.5 = (f32[1,256]{1,0:T(1,128)S(1)}, f32[1,256]{1,0:T(1,128)}, u32[]{:S(2)}) copy-start(f32[1,256]{1,0:T(1,128)} %param.20) | copy-start | bytes 3076
  12.2 108.8 %copy-start.1 = (f32[1,256]{1,0:T(1,128)}, f32[1,256]{1,0:T(1,128)S(1)}, u32[]{:S(2)}) copy-start(f32[1,256]{1,0:T(1,128)S(1)} %dynamic-slice_multiply_fusion.1) | copy-start | bytes 3076
  69.1 51.9 %copy-start.2 = (f32[256]{0:T(256)}, f32[256]{0:T(256)S(1)}, u32[]{:S(2)}) copy-start(f32[256]{0:T(256)S(1)} %subtract_multiply_fusion) | copy-start | bytes 3076
where the time goes:
time: 123 us; the launch traced here: 122 us
  blocking collectives  83.5 us (68%)
  between operations  11.8 us (10%)
  local copies, waits for them, and re-layouts  11.5 us (9%)
  matrix products  8.29 us (7%)
  other arithmetic  6.61 us (5%)
    psum x1, blocking collectives, shards(): loss_sum = lax.psum(jnp.sum(token_loss), ('seq', 'tensor'))  49.3 us
    all_gather x1, blocking collectives, shards(): lax.all_gather(packed[None], ('seq', 'tensor'), axis=0, tiled=True)  31.7 us
    dot_general x1, matrix products, shards(): jnp.einsum('sth,h->st', hidden, scaled, precision=HIGHEST, preferred_elem...  5.97 us
    another operation x1, local copies, waits for them, and re-layouts, shards(): jnp.stack([offset, slope, jnp.sum(weight, axis=1), jnp.sum(weight * local...  3.84 us
    unnamed x1, blocking collectives  2.47 us

commit v1 on v0

--- a/solution.py
+++ b/solution.py
@@ -90,7 +90,12 @@
         ],
         axis=1,
     )
-    gathered = lax.all_gather(packed[None], ("seq", "tensor"), axis=0, tiled=True)
+    gathered = jnp.concatenate(
+        lax.all_to_all(
+            jnp.stack([packed[None]] * lax.axis_size(("seq", "tensor"))), ("seq", "tensor"), 0, 0
+        ),
+        axis=0,
+    )
     seq_count = lax.axis_size("seq")
     table = gathered.reshape(seq_count, seqs_all, 8)
     start_pair = (jnp.zeros((seqs_all,), jnp.float32), jnp.ones((seqs_all,), jnp.float32))

time: 123 us -> 94.6 us (0.77)
  blocking collectives: 83.5 us -> 43.8 us
  starting transfers between devices: 0 us -> 5.99 us
  waiting for transfers between devices: 0 us -> 5.01 us
  matrix products: 8.29 us -> 5.63 us
  other arithmetic: 6.61 us -> 8.74 us
    all_gather x1 -> x0, blocking collectives: 31.7 us -> none  [shards(): lax.all_gather(packed[None], ('seq', 'tensor'), axis=0, tiled=True)]
    psum x1, blocking collectives: 49.3 us -> 41.3 us  [shards(): loss_sum = lax.psum(jnp.sum(token_loss), ('seq', 'tensor'))]
    all_to_all x0 -> x1, starting transfers between devices: none -> 5.99 us  [shards(): lax.all_to_all(jnp.stack([packed[None]] * lax.axis_size(('seq', 'tensor')...]
    all_to_all x0 -> x1, waiting for transfers between devices: none -> 5.01 us  [shards(): lax.all_to_all(jnp.stack([packed[None]] * lax.axis_size(('seq', 'tensor')...]
    dot_general x1, matrix products: 5.97 us -> 3.34 us  [shards(): jnp.einsum('sth,h->st', hidden, scaled, precision=HIGHEST, preferred_elem...]
    dot_general x1, other arithmetic: 0.91 us -> 3.23 us  [shards(): jnp.einsum('sth,sth->st', hidden, hidden, preferred_element_type=jnp.floa...]
  transfers between devices with their start and end apart: 0 -> 1, of which waited for: 0 -> 1; matrix products, arithmetic and copies ran while one was open for 0% -> 0% of each run, Pallas kernels for 0% -> 0%
where the time goes in v1:
time: 94.6 us; the launch traced here: 93.4 us
  blocking collectives  43.8 us (46%)
  local copies, waits for them, and re-layouts  12.1 us (13%)
  between operations  11.9 us (13%)
  other arithmetic  8.74 us (9%)
  starting transfers between devices  5.99 us (6%)
  matrix products  5.63 us (6%)
  waiting for transfers between devices  5.01 us (5%)
    psum x1, blocking collectives, shards(): loss_sum = lax.psum(jnp.sum(token_loss), ('seq', 'tensor'))  41.3 us
    all_to_all x1, starting transfers between devices, shards(): lax.all_to_all(jnp.stack([packed[None]] * lax.axis_size(('seq', 'tensor')...  5.99 us
    all_to_all x1, waiting for transfers between devices, shards(): lax.all_to_all(jnp.stack([packed[None]] * lax.axis_size(('seq', 'tensor')...  5.01 us
    another operation x1, local copies, waits for them, and re-layouts, shards(): jnp.stack([offset, slope, jnp.sum(weight, axis=1), jnp.sum(weight * local...  3.71 us
    dot_general x1, matrix products, shards(): jnp.einsum('sth,h->st', hidden, scaled, precision=HIGHEST, preferred_elem...  3.34 us
    dot_general x1, other arithmetic, shards(): jnp.einsum('sth,sth->st', hidden, hidden, preferred_element_type=jnp.floa...  3.23 us
    unnamed x1, blocking collectives  2.46 us
    dot_general x1, matrix products, local_pass(): jnp.einsum('stj,sj->st', weights, delta, precision=HIGHEST, preferred_ele...  2.29 us
  transfers between devices with their start and end apart: 1, of which 1 were waited for; matrix products, arithmetic and copies ran while one was open for 0% of the time, Pallas kernels for 0%

profile of v1, /device:TPU:12, one launch (start us, length us, event | category | flops | bytes accessed | tf_op | source)
XLA Modules:
  0.0 93.4 jit_solution(14573664629700112390)
XLA Ops:
  0.6 0.0 copy-start
  0.6 0.0 copy-start.1
  0.7 0.0 copy-start.12
  0.7 0.0 copy-start.10
  0.7 0.0 copy-start.7
  0.7 0.0 copy-start.11
  0.7 0.0 copy-start.4
  0.7 0.0 copy-start.9
  0.7 0.0 copy-start.8
  0.7 0.0 copy-start.5
  0.7 0.0 copy-start.6
  0.8 3.2 %fusion.3 = f32[2,256]{1,0:T(2,128)S(1)} fusion(bf16[2,256,4096]{2,1,0:T(8,128)(2,1)} %param.13), kind=kLoop, calls=%fused_computation.9 | loop fusion | flops 6290944 | bytes 4196352 | tf_op jit(solution)/shard_map/sth,sth->st/dot_general | solution.py:59
  4.0 0.0 copy-done.1
  4.0 0.7 convert_multiply_fusion.1
  4.7 0.0 copy-done
  4.7 3.3 %fusion.45 = f32[1,2,256]{2,0,1:T(1,128)S(1)} fusion(f32[4096,1,1]{0,1,2:T(1,128)S(1)} %bitcast.83, bf16[2,256,4096]{2,1,0:T(8,128)(2,1)S(1)} %copy-done), kind=kOutput, calls=%fused_computation.75 | convolution fusion | flops 25165824 | bytes 4212736 | tf_op jit(solution)/shard_map/sth,h->st/dot_general | solution.py:60
  8.0 2.5 %all-reduce.2 = (f32[2,256]{1,0:T(2,128)S(1)}, f32[2,256]{1,0:T(2,128)S(1)}) all-reduce(f32[2,256]{1,0:T(2,128)S(1)} %bitcast.85, f32[2,256]{1,0:T(2,128)S(1)} %fusion.3), channel_id=2, replica_groups=mesh['seq'=16,'tensor'=2] {'tensor'}, use_global_device_ids=true, to_apply=%region_0.0.clone | all-reduce | flops 1024 | bytes 8192
  10.5 0.0 copy-done.12
  10.5 0.6 dynamic-slice.1
  11.1 0.7 dynamic-slice_multiply_fusion.1
  11.8 0.0 copy-start.2
  11.8 0.1 slice.64
  11.8 0.6 slice.67
  12.4 0.0 copy-done.10
  12.4 0.6 dynamic_slice.37
  13.0 0.0 copy-done.7
  13.0 0.6 slice.66
  13.6 0.0 copy-done.11
  13.6 0.6 dynamic_slice.38
  16.8 0.3 reduce-window.6
  17.1 0.2 slice_reduce_fusion.1
  17.3 0.2 reduce-window.9
  17.5 0.1 broadcast.119
  17.6 0.6 slice.65
  18.2 0.0 copy-done.4
  18.2 0.0 copy-done.9
  18.2 2.3 %multiply_reduce_fusion = (f32[]{:T(128)}, f32[]{:T(128)}, f32[]{:T(128)}, f32[]{:T(128)}, f32[]{:T(128)}, /*index=5*/f32[]{:T(128)}, f32[1,256,1]{1,2,0:T(1,128)S(1)}, f32[1,256]{1,0:T(1,128)S(1)}) fusion(s32[1,256]{1,0:T(1,128)S(1)} %copy-done.4, f32[]{:T(128)} %bitcast.13, f32[]{:T(128)} %bitcast.7, s32[256]{0:T(256)S(1)} %bitcast.96, s32[1]{0:T(128)} %slice.65, ...), kind=kOutput, calls=%fused_computation.56 | convolution fusion | flops 1318138 | bytes 13340 | tf_op jit(solution)/shard_map/stj,sj->st/dot_general | solution.py:31
  20.5 0.5 slice.68
  22.3 0.5 slice.69
  24.8 3.7 %stack.40 = f32[1,8]{1,0:T(1,128)S(1)} concatenate(f32[1,1]{1,0:T(1,128)} %bitcast.16, f32[1,1]{1,0:T(1,128)} %bitcast.19, f32[1,1]{1,0:T(1,128)} %bitcast.20, f32[1,1]{1,0:T(1,128)} %bitcast.21, f32[1,1]{1,0:T(1,128)} %bitcast.22, f32[1,1]{1,0:T(1,128)} %bitcast.23, f32[1,1]{1,0:T(1,128)} %bitcast.24, f32[1,1]{1,0:T(1,128)} %bitcast.25), dimensions={1} | concatenate | bytes 64 | tf_op jit(solution)/shard_map/stack | solution.py:80
  28.5 0.6 stack.42
  29.1 6.0 %all-to-all-start = ((f32[32,1,1,8]{3,2,1,0:T(1,128)}), f32[32,1,1,8]{3,2,1,0:T(1,128)S(1)}, u32[]{:S(2)}, u32[]{:S(2)}) async-start(f32[32,1,1,8]{3,2,1,0:T(1,128)} %stack.42), calls=%async_computation | async-start | bytes 32768 | tf_op jit(solution)/shard_map/all_to_all | solution.py:94
  35.1 5.0 %all-to-all-done = f32[32,1,1,8]{3,2,1,0:T(1,128)S(1)} async-done(((f32[32,1,1,8]{3,2,1,0:T(1,128)}), f32[32,1,1,8]{3,2,1,0:T(1,128)S(1)}, u32[]{:S(2)}, u32[]{:S(2)}) %all-to-all-start) | async-done | bytes 1056 | tf_op jit(solution)/shard_map/all_to_all | solution.py:94
  40.1 0.7 slice_reduce_fusion
  40.8 0.1 copy.37
  40.9 0.1 copy.36
  41.0 0.1 copy.40
  41.1 0.1 copy.39
  41.2 0.1 copy.38
  41.3 0.1 copy.30
  41.4 0.1 copy.32
  41.5 0.1 copy.31
  41.6 0.1 copy.33
  41.7 1.8 %while.21 = (s32[]{:T(128)}, f32[2]{0:T(128)S(1)}, f32[2]{0:T(128)S(1)}, f32[16,2]{1,0:T(8,128)S(1)}, f32[16,2]{1,0:T(8,128)S(1)}, /*index=5*/f32[16,2]{1,0:T(8,...) while((s32[]{:T(128)}, f32[2]{0:T(128)S(1)}, f32[2]{0:T(128)S(1)}, ...), condition=%wide.region_11.12_spmd.clone, body=%wide.region_10.11_spmd.clone.sunk | while | flops 14 | bytes 239 | solution.py:102
  43.5 0.1 copy.35
  43.6 0.1 copy.34
  43.6 0.0 copy-done.8
  43.6 0.7 fusion.34
  44.3 0.7 dynamic_slice.40
  45.0 0.7 broadcast_multiply_fusion
  48.4 0.0 copy-start.3
  48.4 0.0 copy-done.5
  48.4 1.3 %fusion.43 = (f32[]{:T(128)}, f32[1,256]{1,0:T(1,128)}) fusion(f32[1,256]{1,0:T(1,128)S(1)} %bitcast.90, f32[1,256]{1,0:T(1,128)S(1)} %copy-done.5, f32[1,256]{1,0:T(1,128)S(1)} %copy-done.6, s32[1,256]{1,0:T(1,128)S(1)} %copy-done.4), kind=kLoop, calls=%fused_computation.74 | loop fusion | flops 2303 | bytes 5124 | tf_op jit(solution)/shard_map/reduce_sum | solution.py:119
  49.7 41.3 %psum.7 = f32[]{:T(128)} all-reduce(f32[]{:T(128)} %get-tuple-element.217), channel_id=1, replica_groups=mesh['seq'=16,'tensor'=2] {'seq','tensor'}, use_global_device_ids=true, to_apply=%region_16.17 | all-reduce | flops 1 | bytes 8 | tf_op jit(solution)/shard_map/psum | solution.py:119
  (60 shorter events, 1.5 us)
Async XLA Ops:
  0.6 4.1 %copy-start = (bf16[2,256,4096]{2,1,0:T(8,128)(2,1)S(1)}, bf16[2,256,4096]{2,1,0:T(8,128)(2,1)}, u32[]{:S(2)}) copy-start(bf16[2,256,4096]{2,1,0:T(8,128)(2,1)} %param.13) | copy-start | bytes 12582916
  0.6 3.3 %copy-start.1 = (bf16[4096]{0:T(1024)(128)(2,1)S(1)}, bf16[4096]{0:T(1024)(128)(2,1)}, u32[]{:S(2)}) copy-start(bf16[4096]{0:T(1024)(128)(2,1)} %param.15) | copy-start | bytes 24580
  0.7 9.8 %copy-start.12 = (u32[32]{0:T(128)S(1)}, u32[32]{0:T(128)}, u32[]{:S(2)}) copy-start(u32[32]{0:T(128)} %constant.101) | copy-start | bytes 388
  0.7 11.8 %copy-start.10 = (f32[2]{0:T(128)S(1)}, f32[2]{0:T(128)}, u32[]{:S(2)}) copy-start(f32[2]{0:T(128)} %param.21) | copy-start | bytes 28
  0.7 12.3 %copy-start.7 = (s32[2,256]{1,0:T(2,128)S(1)}, s32[2,256]{1,0:T(2,128)}, u32[]{:S(2)}) copy-start(s32[2,256]{1,0:T(2,128)} %param.17) | copy-start | bytes 6148
  0.7 12.9 %copy-start.11 = (f32[2]{0:T(128)S(1)}, f32[2]{0:T(128)}, u32[]{:S(2)}) copy-start(f32[2]{0:T(128)} %param.22) | copy-start | bytes 28
  0.7 17.5 %copy-start.4 = (s32[1,256]{1,0:T(1,128)S(1)}, s32[1,256]{1,0:T(1,128)}, u32[]{:S(2)}) copy-start(s32[1,256]{1,0:T(1,128)} %param.18) | copy-start | bytes 3076
  0.7 17.5 %copy-start.9 = (f32[2,256]{1,0:T(2,128)S(1)}, f32[2,256]{1,0:T(2,128)}, u32[]{:S(2)}) copy-start(f32[2,256]{1,0:T(2,128)} %param.16) | copy-start | bytes 6148
  0.7 42.9 %copy-start.8 = (f32[2]{0:T(128)S(1)}, f32[2]{0:T(128)}, u32[]{:S(2)}) copy-start(f32[2]{0:T(128)} %param.23) | copy-start | bytes 28
  0.7 47.7 %copy-start.5 = (f32[1,256]{1,0:T(1,128)S(1)}, f32[1,256]{1,0:T(1,128)}, u32[]{:S(2)}) copy-start(f32[1,256]{1,0:T(1,128)} %param.19) | copy-start | bytes 3076
  0.7 47.7 %copy-start.6 = (f32[1,256]{1,0:T(1,128)S(1)}, f32[1,256]{1,0:T(1,128)}, u32[]{:S(2)}) copy-start(f32[1,256]{1,0:T(1,128)} %param.20) | copy-start | bytes 3076
  11.8 80.5 %copy-start.2 = (f32[1,256]{1,0:T(1,128)}, f32[1,256]{1,0:T(1,128)S(1)}, u32[]{:S(2)}) copy-start(f32[1,256]{1,0:T(1,128)S(1)} %dynamic-slice_multiply_fusion.1) | copy-start | bytes 3076
  29.1 11.0 %all-to-all-start = ((f32[32,1,1,8]{3,2,1,0:T(1,128)}), f32[32,1,1,8]{3,2,1,0:T(1,128)S(1)}, u32[]{:S(2)}, u32[]{:S(2)}) async-start(f32[32,1,1,8]{3,2,1,0:T(1,128)} %stack.42), calls=%async_computation | async-start | bytes 32768 | tf_op jit(solution)/shard_map/all_to_all | solution.py:94
  48.4 43.9 %copy-start.3 = (f32[256]{0:T(256)}, f32[256]{0:T(256)S(1)}, u32[]{:S(2)}) copy-start(f32[256]{0:T(256)S(1)} %subtract_multiply_fusion) | copy-start | bytes 3076
